TPU v7x, 32 devices: a whole 2x2x4 slice. The times are simulated.
32 devices in a mesh: kpt: 2 (over x), px: 16 (over z, y, core).
Axes of the slice: x: 2, y: 2, z: 4, core: 2. Of those that a mesh axis runs over, the one named last changes fastest.
Arguments:
- right_side: float32 [2, 3, 2, 64, 4096], P(None, None, 'kpt', 'px'), parts along dimension 2, may hold values from -6 to 6
- material: int32 [64, 4096], P('px'), may hold values from 0 to 2
- permittivity: float32 [3], replicated, may hold values from 1 to 2
- bloch_phase: float32 [6], P('kpt'), parts along dimension 0, may hold values from -3.140625 to 3.140625
- quad_shift: float32 [2], replicated, may hold values from 0.05 to 0.6, as said below
Outputs:
- solution: float32 [2, 3, 2, 64, 4096], P(None, None, 'kpt', 'px'), parts along dimension 2
- residual: float32 [2, 3, 2, 64, 4096], P(None, None, 'kpt', 'px'), parts along dimension 2
There are 2 independent parts, one for each index of `kpt`. A program takes and returns all parts, laid end to end along the dimension named above; an argument that names none is the same for every part. Nothing has to cross between parts.
Inputs may be any that keep to these rules, and one draw needn't show every extreme that they name: quad_shift[0] lies in 0.05 to 0.1 and quad_shift[1] in 0.3 to 0.6.
All inputs are finite; a program needn't handle non-finite values.
Results may differ from a plain program's by a relative error of at most 0.0003.
Values sent between devices are 32-bit elements; how exact they have to be, the bound alone decides.
A program may use at most 128 MiB of HBM per device.

v0:
```python
import math
import jax
import jax.numpy as jnp
from jax import lax
from jax.sharding import PartitionSpec as P

NG = 64
ITERS = 3
PRECISE = lax.Precision.HIGHEST


def from_behind(value, axis, steps):
    count = lax.axis_size(axis)
    pairs = [(source, (source + steps) % count) for source in range(count)]
    return lax.ppermute(value, axis, pairs)


def padded(shard, sides, width):
    for axis, dim in sides:
        size, length = (lax.axis_size(axis), shard.shape[dim])
        up = [(i, (i + 1) % size) for i in range(size)]
        down = [(j, i) for i, j in up]
        last = lax.slice_in_dim(shard, length - width, length, axis=dim)
        first = lax.slice_in_dim(shard, 0, width, axis=dim)
        before = lax.ppermute(last, axis, up)
        after = lax.ppermute(first, axis, down)
        shard = jnp.concatenate([before, shard, after], axis=dim)
    return shard


def block_solve(matrix_re, matrix_im, right_re, right_im):
    blocks = matrix_re.shape[0]
    system = jnp.concatenate(
        [jnp.concatenate([matrix_re, -matrix_im], 1), jnp.concatenate([matrix_im, matrix_re], 1)], 0
    )
    values = jnp.concatenate([right_re, right_im], 0)
    doubled = 2 * blocks
    pivot_row = 0
    factors = system[pivot_row + 1 :, pivot_row : pivot_row + 1] / system[pivot_row, pivot_row]
    system = jnp.concatenate(
        [
            system[: pivot_row + 1],
            system[pivot_row + 1 :] - factors * system[pivot_row : pivot_row + 1],
        ],
        0,
    )
    values = jnp.concatenate(
        [
            values[: pivot_row + 1],
            values[pivot_row + 1 :] - factors * values[pivot_row : pivot_row + 1],
        ],
        0,
    )
    rows_out = [None] * doubled
    for pivot_row in range(doubled - 1, -1, -1):
        running = values[pivot_row]
        for later_row in range(pivot_row + 1, doubled):
            running = running - system[pivot_row, later_row] * rows_out[later_row]
        rows_out[pivot_row] = running / system[pivot_row, pivot_row]
    solved = jnp.stack(rows_out, 0)
    return (solved[:blocks], solved[blocks:])


def material_scale(material, permittivity):
    scaled = jnp.zeros(material.shape, jnp.float32)
    for material_id in range(permittivity.shape[0]):
        scaled = scaled + jnp.where(
            material == material_id, permittivity[material_id], jnp.float32(0.0)
        )
    return scaled


def rotate(fields, cosine, sine_part):
    return jnp.stack(
        [cosine * fields[0] - sine_part * fields[1], sine_part * fields[0] + cosine * fields[1]]
    )


def edge_mask(fields, along, target):
    layout = tuple(
        (fields.shape[place_dim] if place_dim == along else 1 for place_dim in range(fields.ndim))
    )
    return lax.broadcasted_iota(jnp.int32, layout, along) == target


def forward_step(fields, along, cosine, sine_part):
    rolled = jnp.roll(fields, -1, along)
    return (
        jnp.where(
            edge_mask(fields, along, fields.shape[along] - 1),
            rotate(rolled, cosine, sine_part),
            rolled,
        )
        - fields
    )


def backward_step(fields, along, cosine, sine_part):
    rolled = jnp.roll(fields, 1, along)
    return (
        jnp.where(edge_mask(fields, along, 0), rotate(rolled, cosine, -sine_part), rolled) - fields
    )


def next_step(fields, upper_next):
    return jnp.concatenate([fields[:, :, 1:], upper_next], 2) - fields


def prior_step(fields, lower_prev):
    return jnp.concatenate([lower_prev, fields[:, :, :-1]], 2) - fields


def curl(fields, upper_next, turn_values):
    cosine_y, sine_y, cosine_z, sine_z = turn_values
    first = forward_step(fields[:, 2], 3, cosine_y, sine_y) - forward_step(
        fields[:, 1], 4, cosine_z, sine_z
    )
    second = forward_step(fields[:, 0], 4, cosine_z, sine_z) - next_step(
        fields[:, 2], upper_next[:, 1]
    )
    third = next_step(fields[:, 1], upper_next[:, 0]) - forward_step(
        fields[:, 0], 3, cosine_y, sine_y
    )
    return jnp.stack([first, second, third], 1)


def curl_adjoint(fields, lower_prev, turn_values):
    cosine_y, sine_y, cosine_z, sine_z = turn_values
    first = backward_step(fields[:, 1], 4, cosine_z, sine_z) - backward_step(
        fields[:, 2], 3, cosine_y, sine_y
    )
    second = prior_step(fields[:, 2], lower_prev[:, 1]) - backward_step(
        fields[:, 0], 4, cosine_z, sine_z
    )
    third = backward_step(fields[:, 0], 3, cosine_y, sine_y) - prior_step(
        fields[:, 1], lower_prev[:, 0]
    )
    return jnp.stack([first, second, third], 1)


def transform_table(theta_value, forward):
    row_index = lax.broadcasted_iota(jnp.int32, (NG, NG), 0)
    col_index = lax.broadcasted_iota(jnp.int32, (NG, NG), 1)
    angles = (
        2.0 * math.pi * (row_index * col_index % NG).astype(jnp.float32) / NG
        + theta_value * col_index.astype(jnp.float32) / NG
    )
    if forward:
        return (jnp.cos(angles), -jnp.sin(angles))
    return (jnp.cos(angles) / NG, jnp.sin(angles) / NG)


def contract(fields, tables, pattern):
    real_part = jnp.einsum(pattern, fields[0], tables[0], precision=PRECISE) - jnp.einsum(
        pattern, fields[1], tables[1], precision=PRECISE
    )
    imag_part = jnp.einsum(pattern, fields[0], tables[1], precision=PRECISE) + jnp.einsum(
        pattern, fields[1], tables[0], precision=PRECISE
    )
    return jnp.stack([real_part, imag_part])


def column_symbol(fields, bloch_phase, damping, col_start):
    length_axis = fields.shape[4]
    mode_index = lax.broadcasted_iota(jnp.int32, (NG, 1), 0).astype(jnp.float32)
    columns = col_start + lax.broadcasted_iota(jnp.int32, (1, length_axis), 1)
    kappa_x = (2.0 * math.pi * mode_index + bloch_phase[0]) / NG
    kappa_y = (2.0 * math.pi * (columns // NG).astype(jnp.float32) + bloch_phase[1]) / NG
    kappa_z = (2.0 * math.pi * (columns % NG).astype(jnp.float32) + bloch_phase[2]) / NG
    differences = [(jnp.cos(kappa) - 1.0, jnp.sin(kappa)) for kappa in (kappa_x, kappa_y, kappa_z)]
    inner_re = sum(
        (
            differences[which_one][0] * fields[0, which_one]
            + differences[which_one][1] * fields[1, which_one]
            for which_one in range(3)
        )
    )
    inner_im = sum(
        (
            differences[which_one][0] * fields[1, which_one]
            - differences[which_one][1] * fields[0, which_one]
            for which_one in range(3)
        )
    )
    magnitude = sum(
        (differences[which_one][0] ** 2 + differences[which_one][1] ** 2 for which_one in range(3))
    )
    outputs = []
    for which_one in range(3):
        diff_re, diff_im = differences[which_one]
        out_re = (fields[0, which_one] + (diff_re * inner_re - diff_im * inner_im) / damping) / (
            magnitude + damping
        )
        out_im = (fields[1, which_one] + (diff_re * inner_im + diff_im * inner_re) / damping) / (
            magnitude + damping
        )
        outputs.append(jnp.stack([out_re, out_im]))
    return jnp.stack(outputs, 1)


def gram(left_side, right_part):
    pattern = "cvxn,cwxn->vw"
    real_part = jnp.einsum(pattern, left_side[0], right_part[0], precision=PRECISE) + jnp.einsum(
        pattern, left_side[1], right_part[1], precision=PRECISE
    )
    imag_part = jnp.einsum(pattern, left_side[0], right_part[1], precision=PRECISE) - jnp.einsum(
        pattern, left_side[1], right_part[0], precision=PRECISE
    )
    return (real_part, imag_part)


def mix(fields, step_coef):
    pattern = "cvxn,vw->cwxn"
    real_part = jnp.einsum(pattern, fields[0], step_coef[0], precision=PRECISE) - jnp.einsum(
        pattern, fields[1], step_coef[1], precision=PRECISE
    )
    imag_part = jnp.einsum(pattern, fields[0], step_coef[1], precision=PRECISE) + jnp.einsum(
        pattern, fields[1], step_coef[0], precision=PRECISE
    )
    return jnp.stack([real_part, imag_part])


def on_device(right_side, material, permittivity, bloch_phase, quad_shift):
    vectors = right_side.shape[2]
    planes = right_side.shape[3]
    position = lax.axis_index("px")
    last_device = lax.axis_size("px") - 1
    permit = material_scale(material, permittivity).reshape(planes, NG, NG)
    inverse_eps = 1.0 / permit
    lower_kind = from_behind(material[-1:], "px", 1)
    inverse_lower = 1.0 / material_scale(lower_kind, permittivity).reshape(1, NG, NG)
    damping = quad_shift[0] * jnp.mean(permittivity)
    turn_values = (
        jnp.cos(bloch_phase[1]),
        jnp.sin(bloch_phase[1]),
        jnp.cos(bloch_phase[2]),
        jnp.sin(bloch_phase[2]),
    )
    is_top = position == last_device
    is_bottom = position == 0
    cosine_up = jnp.where(is_top, jnp.cos(bloch_phase[0]), 1.0)
    sine_up = jnp.where(is_top, jnp.sin(bloch_phase[0]), 0.0)
    cosine_down = jnp.where(is_bottom, jnp.cos(bloch_phase[0]), 1.0)
    sine_down = jnp.where(is_bottom, -jnp.sin(bloch_phase[0]), 0.0)
    forward_tables = [transform_table(bloch_phase[which_one], True) for which_one in range(3)]
    inverse_tables = [transform_table(bloch_phase[which_one], False) for which_one in range(3)]
    columns = NG * NG // lax.axis_size("px")
    col_start = position * columns

    def column_work(pieces):
        spectrum = contract(pieces, forward_tables[0], "cvjn,mj->cvmn")
        spectrum = column_symbol(spectrum, bloch_phase, damping, col_start)
        return contract(spectrum, inverse_tables[0], "cvmn,mj->cvjn")

    def precondition(flat_field):
        fields = flat_field.reshape(2, 3, vectors, planes, NG, NG)
        fields = contract(fields, forward_tables[2], "cvxyj,mj->cvxym")
        fields = contract(fields, forward_tables[1], "cvxjz,mj->cvxmz")
        flat_spectrum = fields.reshape(2, 3, vectors, planes, NG * NG)
        gathered = lax.all_to_all(flat_spectrum, "px", split_axis=4, concat_axis=3, tiled=True)
        worked = column_work(gathered)
        returned = lax.all_to_all(worked, "px", split_axis=3, concat_axis=4, tiled=True)
        fields = returned.reshape(2, 3, vectors, planes, NG, NG)
        fields = contract(fields, inverse_tables[1], "cvxmz,mj->cvxjz")
        fields = contract(fields, inverse_tables[2], "cvxym,mj->cvxyj")
        return fields.reshape(flat_field.shape)

    solution = jnp.zeros_like(right_side)
    residual = right_side
    direction = precondition(residual)
    for iteration in range(ITERS):
        operate_fields = direction.reshape(2, 3, direction.shape[2], planes, NG, NG)
        extended = padded(operate_fields, (("px", 3),), 1)
        bottom = rotate(extended[:, :, :, :1], cosine_down, sine_down)
        top_plane = rotate(extended[:, :, :, -1:], cosine_up, sine_up)
        extended = jnp.concatenate([bottom, extended[:, :, :, 1:-1], top_plane], 3)
        curled = curl(
            extended[:, :, :, :-1], extended[:, 1:3, :, -1:], turn_values
        ) * jnp.concatenate([inverse_lower, inverse_eps], 0)
        result = curl_adjoint(curled[:, :, :, 1:], curled[:, 1:3, :, :1], turn_values)
        mass_term = rotate(operate_fields, quad_shift[0], quad_shift[1]) * permit
        image_dir = (result + mass_term).reshape(direction.shape)
        first_pair = gram(direction, image_dir)
        second_pair = gram(direction, residual)
        totals = lax.psum((first_pair[0], first_pair[1], second_pair[0], second_pair[1]), "px")
        step_coef = block_solve(totals[0], totals[1], totals[2], totals[3])
        solution = solution + mix(direction, step_coef)
        residual = residual - mix(image_dir, step_coef)
        if iteration < ITERS - 1:
            precond = precondition(residual)
            update_pair = gram(image_dir, precond)
            update_totals = lax.psum((update_pair[0], update_pair[1]), "px")
            beta_re, beta_im = block_solve(totals[0], totals[1], update_totals[0], update_totals[1])
            direction = precond + mix(direction, (-beta_re, -beta_im))
    return (solution, residual)


def solution(mesh):
    return jax.shard_map(
        on_device,
        mesh=mesh,
        in_specs=(P(None, None, "kpt", "px", None), P("px", None), P(), P("kpt"), P()),
        out_specs=(P(None, None, "kpt", "px", None), P(None, None, "kpt", "px", None)),
        check_vma=False,
    )
```

profile of v0, /device:TPU:0, one launch (start us, length us, event | category | flops | bytes accessed | tf_op | source)
XLA Modules:
  0.0 819.2 jit_solution(17893291572140384924)
XLA Ops:
  17.2 10.4 %copy.2218 = f32[1,3,1,4,4096]{3,0,2,1,4:T(1,128)} copy(f32[1,3,1,4,4096]{4,3,1,2,0:T(4,128)S(1)} %stack.595) | data formatting | bytes 393216 | tf_op jit(solution)/shard_map/stack | solution.py:160
  27.6 10.1 %copy.2219 = f32[1,3,1,4,4096]{3,0,2,1,4:T(1,128)} copy(f32[1,3,1,4,4096]{4,3,1,2,0:T(4,128)S(1)} %stack.596) | data formatting | bytes 393216 | tf_op jit(solution)/shard_map/stack | solution.py:160
  37.7 16.6 %fusion.762 = f32[4096,3,1,2,4]{4,3,2,1,0:T(2,128)} fusion(f32[1,3,1,4,4096]{3,0,2,1,4:T(1,128)} %copy.2219, f32[1,3,1,4,4096]{3,0,2,1,4:T(1,128)} %copy.2218), kind=kLoop, calls=%fused_computation.1223 | loop fusion | flops 98304 | bytes 786432
  54.4 17.6 %reshape.14430 = f32[16,1,6144]{2,1,0:T(1,128)} reshape(f32[4096,3,1,2,4]{4,3,2,1,0:T(2,128)} %fusion.762) | data formatting | bytes 786432
  72.0 7.2 all-to-all-start
  86.4 5.0 all-to-all-done
  93.4 24.8 %reshape.14431 = f32[4096,3,1,2,4]{4,3,2,1,0:T(2,128)} reshape(f32[16,6144]{1,0:T(8,128)S(1)} %reduce.68) | data formatting | bytes 786432
  118.2 15.5 %copy.2220 = f32[2,3,1,4,16,256]{5,3,4,1,2,0:T(4,128)S(1)} copy(f32[2,3,1,4,16,256]{3,0,1,5,4,2:T(2,128)} %bitcast.1769) | data formatting | bytes 786432 | tf_op jit(solution)/shard_map/all_to_all | solution.py:260
  166.5 4.5 collective-permute-start.1
  212.5 32.6 %all-reduce.4 = (f32[1,1]{1,0:T(1,128)}, f32[1,1]{1,0:T(1,128)}, f32[1,1]{1,0:T(1,128)}, f32[1,1]{1,0:T(1,128)}) all-reduce(f32[1,1]{1,0:T(1,128)} %bitcast.259, f32[1,1]{1,0:T(1,128)} %bitcast.256, f32[1,1]{1,0:T(1,128)} %bitcast.260, f32[1,1]{1,0:T(1,128)} %bitcast.154), channel_id=1, replica_groups=mesh['kpt'=2,'px'=16] {'px'}, use_global_device_ids=true, to_apply=%region_3.4 | all-reduce | flops 4 | bytes 32 | tf_op jit(solution)/shard_map/psum | solution.py:285
  259.9 10.4 %copy.2320 = f32[1,3,1,4,4096]{3,0,2,1,4:T(1,128)} copy(f32[1,3,1,4,4096]{4,3,1,2,0:T(4,128)S(1)} %stack.650) | data formatting | bytes 393216 | tf_op jit(solution)/shard_map/stack | solution.py:160
  270.3 10.1 %copy.2321 = f32[1,3,1,4,4096]{3,0,2,1,4:T(1,128)} copy(f32[1,3,1,4,4096]{4,3,1,2,0:T(4,128)S(1)} %stack.651) | data formatting | bytes 393216 | tf_op jit(solution)/shard_map/stack | solution.py:160
  280.5 16.6 %fusion.761 = f32[4096,3,1,2,4]{4,3,2,1,0:T(2,128)} fusion(f32[1,3,1,4,4096]{3,0,2,1,4:T(1,128)} %copy.2321, f32[1,3,1,4,4096]{3,0,2,1,4:T(1,128)} %copy.2320), kind=kLoop, calls=%fused_computation.1222 | loop fusion | flops 98304 | bytes 786432
  297.1 17.0 %reshape.14432 = f32[16,1,6144]{2,1,0:T(1,128)S(1)} reshape(f32[4096,3,1,2,4]{4,3,2,1,0:T(2,128)} %fusion.761) | data formatting | bytes 786432
  314.1 15.2 %all_to_all.90 = f32[16,1,6144]{2,1,0:T(1,128)S(1)} all-to-all(f32[16,1,6144]{2,1,0:T(1,128)S(1)} %reshape.14432), channel_id=1, replica_groups=mesh['kpt'=2,'px'=16] {'px'}, dimensions={0} | all-to-all | bytes 786432 | tf_op jit(solution)/shard_map/all_to_all | solution.py:260
  330.7 24.8 %reshape.14433 = f32[4096,3,1,2,4]{4,3,2,1,0:T(2,128)} reshape(f32[16,6144]{1,0:T(8,128)S(1)} %reduce.69) | data formatting | bytes 786432
  355.5 15.5 %copy.2322 = f32[2,3,1,4,16,256]{5,3,4,1,2,0:T(4,128)S(1)} copy(f32[2,3,1,4,16,256]{3,0,1,5,4,2:T(2,128)} %bitcast.1770) | data formatting | bytes 786432 | tf_op jit(solution)/shard_map/all_to_all | solution.py:260
  375.9 15.5 %all_to_all.91 = f32[2,3,1,64,256]{4,0,2,1,3:T(2,128)S(1)} all-to-all(f32[2,3,1,64,256]{4,0,2,1,3:T(2,128)S(1)} %copy.2339), channel_id=1, replica_groups=mesh['kpt'=2,'px'=16] {'px'}, dimensions={3} | all-to-all | bytes 786432 | tf_op jit(solution)/shard_map/all_to_all | solution.py:262
  401.8 33.2 %all-reduce.3 = (f32[1,1]{1,0:T(1,128)}, f32[1,1]{1,0:T(1,128)}) all-reduce(f32[1,1]{1,0:T(1,128)} %bitcast.335, f32[1,1]{1,0:T(1,128)} %bitcast.334), channel_id=1, replica_groups=mesh['kpt'=2,'px'=16] {'px'}, use_global_device_ids=true, to_apply=%region_6.7 | all-reduce | flops 2 | bytes 16 | tf_op jit(solution)/shard_map/psum | solution.py:292
  444.4 4.6 collective-permute-start.4
  495.1 32.3 %all-reduce.2 = (f32[1,1]{1,0:T(1,128)}, f32[1,1]{1,0:T(1,128)}, f32[1,1]{1,0:T(1,128)}, f32[1,1]{1,0:T(1,128)}) all-reduce(f32[1,1]{1,0:T(1,128)} %bitcast.436, f32[1,1]{1,0:T(1,128)} %bitcast.431, f32[1,1]{1,0:T(1,128)} %bitcast.439, f32[1,1]{1,0:T(1,128)} %bitcast.348), channel_id=1, replica_groups=mesh['kpt'=2,'px'=16] {'px'}, use_global_device_ids=true, to_apply=%region_9.10 | all-reduce | flops 4 | bytes 32 | tf_op jit(solution)/shard_map/psum | solution.py:285
  541.3 10.4 %copy.2435 = f32[1,3,1,4,4096]{3,0,2,1,4:T(1,128)} copy(f32[1,3,1,4,4096]{4,3,1,2,0:T(4,128)S(1)} %stack.714) | data formatting | bytes 393216 | tf_op jit(solution)/shard_map/stack | solution.py:160
  551.7 10.1 %copy.2436 = f32[1,3,1,4,4096]{3,0,2,1,4:T(1,128)} copy(f32[1,3,1,4,4096]{4,3,1,2,0:T(4,128)S(1)} %stack.715) | data formatting | bytes 393216 | tf_op jit(solution)/shard_map/stack | solution.py:160
  561.8 16.6 %fusion.760 = f32[4096,3,1,2,4]{4,3,2,1,0:T(2,128)} fusion(f32[1,3,1,4,4096]{3,0,2,1,4:T(1,128)} %copy.2436, f32[1,3,1,4,4096]{3,0,2,1,4:T(1,128)} %copy.2435), kind=kLoop, calls=%fused_computation.1221 | loop fusion | flops 98304 | bytes 786432
  578.5 17.0 %reshape.14434 = f32[16,1,6144]{2,1,0:T(1,128)S(1)} reshape(f32[4096,3,1,2,4]{4,3,2,1,0:T(2,128)} %fusion.760) | data formatting | bytes 786432
  595.4 14.9 %all_to_all.92 = f32[16,1,6144]{2,1,0:T(1,128)S(1)} all-to-all(f32[16,1,6144]{2,1,0:T(1,128)S(1)} %reshape.14434), channel_id=1, replica_groups=mesh['kpt'=2,'px'=16] {'px'}, dimensions={0} | all-to-all | bytes 786432 | tf_op jit(solution)/shard_map/all_to_all | solution.py:260
  611.9 24.8 %reshape.14435 = f32[4096,3,1,2,4]{4,3,2,1,0:T(2,128)} reshape(f32[16,6144]{1,0:T(8,128)S(1)} %reduce.70) | data formatting | bytes 786432
  636.7 15.5 %copy.2437 = f32[2,3,1,4,16,256]{5,3,4,1,2,0:T(4,128)S(1)} copy(f32[2,3,1,4,16,256]{3,0,1,5,4,2:T(2,128)} %bitcast.1771) | data formatting | bytes 786432 | tf_op jit(solution)/shard_map/all_to_all | solution.py:260
  657.1 15.5 %all_to_all.93 = f32[2,3,1,64,256]{4,0,2,1,3:T(2,128)S(1)} all-to-all(f32[2,3,1,64,256]{4,0,2,1,3:T(2,128)S(1)} %copy.2442), channel_id=1, replica_groups=mesh['kpt'=2,'px'=16] {'px'}, dimensions={3} | all-to-all | bytes 786432 | tf_op jit(solution)/shard_map/all_to_all | solution.py:262
  682.4 33.4 %all-reduce.1 = (f32[1,1]{1,0:T(1,128)}, f32[1,1]{1,0:T(1,128)}) all-reduce(f32[1,1]{1,0:T(1,128)} %bitcast.501, f32[1,1]{1,0:T(1,128)} %bitcast.500), channel_id=1, replica_groups=mesh['kpt'=2,'px'=16] {'px'}, use_global_device_ids=true, to_apply=%region_12.13 | all-reduce | flops 2 | bytes 16 | tf_op jit(solution)/shard_map/psum | solution.py:292
  727.9 4.6 collective-permute-start.6
  777.2 32.3 %all-reduce = (f32[1,1]{1,0:T(1,128)}, f32[1,1]{1,0:T(1,128)}, f32[1,1]{1,0:T(1,128)}, f32[1,1]{1,0:T(1,128)}) all-reduce(f32[1,1]{1,0:T(1,128)} %bitcast.589, f32[1,1]{1,0:T(1,128)} %bitcast.584, f32[1,1]{1,0:T(1,128)} %bitcast.592, f32[1,1]{1,0:T(1,128)} %bitcast.514), channel_id=1, replica_groups=mesh['kpt'=2,'px'=16] {'px'}, use_global_device_ids=true, to_apply=%region_15.16 | all-reduce | flops 4 | bytes 32 | tf_op jit(solution)/shard_map/psum | solution.py:285
  (733 shorter events, 232.7 us)
Async XLA Ops:
  1.5 148.7 %collective-permute-start.2 = (s32[1,4096]{1,0:T(1,128)S(1)}, s32[1,4096]{1,0:T(1,128)S(1)}, u32[]{:S(2)}, u32[]{:S(2)}) collective-permute-start(s32[1,4096]{1,0:T(1,128)S(1)} %slice.1041), channel_id=1, source_target_pairs={{0,1},{1,2},{2,3},{3,4},{4,5},{5,6},{6,7},{7,8},{8,9},{9,10},{10,1... | collective-permute-start | bytes 49160 | tf_op jit(solution)/shard_map/ppermute | solution.py:15
  4.1 393.6 %copy-start.96 = (f32[64]{0:T(128)}, f32[64]{0:T(128)S(1)}, u32[]{:S(2)}) copy-start(f32[64]{0:T(128)S(1)} %multiply_multiply_fusion) | copy-start | bytes 772
  8.6 386.4 %copy-start.98 = (f32[64]{0:T(128)}, f32[64]{0:T(128)S(1)}, u32[]{:S(2)}) copy-start(f32[64]{0:T(128)S(1)} %multiply_multiply_fusion.2) | copy-start | bytes 772
  72.0 19.4 %all-to-all-start = ((f32[16,1,6144]{2,1,0:T(1,128)}), f32[16,1,6144]{2,1,0:T(1,128)S(1)}, u32[]{:S(2)}, u32[]{:S(2)}) async-start(f32[16,1,6144]{2,1,0:T(1,128)} %reshape.14430), calls=%async_computation | async-start | bytes 786432 | tf_op jit(solution)/shard_map/all_to_all | solution.py:260
  82.3 53.7 %copy-start.126 = (f32[64]{0:T(128)}, f32[64]{0:T(128)S(1)}, u32[]{:S(2)}) copy-start(f32[64]{0:T(128)S(1)} %get-tuple-element.318) | copy-start | bytes 772
  82.3 53.7 %copy-start.129 = (f32[64]{0:T(128)}, f32[64]{0:T(128)S(1)}, u32[]{:S(2)}) copy-start(f32[64]{0:T(128)S(1)} %get-tuple-element.319) | copy-start | bytes 772
  83.0 53.0 %copy-start.132 = (f32[64]{0:T(128)}, f32[64]{0:T(128)S(1)}, u32[]{:S(2)}) copy-start(f32[64]{0:T(128)S(1)} %get-tuple-element.321) | copy-start | bytes 772
  83.0 292.1 %copy-start.100 = (f32[64]{0:T(128)}, f32[64]{0:T(128)S(1)}, u32[]{:S(2)}) copy-start(f32[64]{0:T(128)S(1)} %get-tuple-element.320) | copy-start | bytes 772
  84.3 288.9 %copy-start.109 = (f32[256]{0:T(256)}, f32[256]{0:T(256)S(1)}, u32[]{:S(2)}) copy-start(f32[256]{0:T(256)S(1)} %get-tuple-element.323) | copy-start | bytes 3076
  84.3 288.9 %copy-start.111 = (f32[256]{0:T(256)}, f32[256]{0:T(256)S(1)}, u32[]{:S(2)}) copy-start(f32[256]{0:T(256)S(1)} %get-tuple-element.322) | copy-start | bytes 3076
  85.0 288.2 %copy-start.113 = (f32[256]{0:T(256)}, f32[256]{0:T(256)S(1)}, u32[]{:S(2)}) copy-start(f32[256]{0:T(256)S(1)} %get-tuple-element.314) | copy-start | bytes 3076
  85.0 288.2 %copy-start.115 = (f32[256]{0:T(256)}, f32[256]{0:T(256)S(1)}, u32[]{:S(2)}) copy-start(f32[256]{0:T(256)S(1)} %get-tuple-element.315) | copy-start | bytes 3076
  85.7 287.6 %copy-start.117 = (f32[256]{0:T(256)}, f32[256]{0:T(256)S(1)}, u32[]{:S(2)}) copy-start(f32[256]{0:T(256)S(1)} %get-tuple-element.316) | copy-start | bytes 3076
  85.7 287.6 %copy-start.119 = (f32[256]{0:T(256)}, f32[256]{0:T(256)S(1)}, u32[]{:S(2)}) copy-start(f32[256]{0:T(256)S(1)} %get-tuple-element.317) | copy-start | bytes 3076
  139.3 16.1 %all-to-all-start.1 = ((f32[2,3,1,64,256]{4,0,2,1,3:T(2,128)}), f32[2,3,1,64,256]{4,0,2,1,3:T(2,128)S(1)}, u32[]{:S(2)}, u32[]{:S(2)}) async-start(f32[2,3,1,64,256]{4,0,2,1,3:T(2,128)} %copy.2232), calls=%async_computation.1 | async-start | bytes 786432 | tf_op jit(solution)/shard_map/all_to_all | solution.py:262
  145.4 59.1 %copy-start.20 = (f32[4,64,64]{2,1,0:T(8,128)}, f32[4,64,64]{2,1,0:T(8,128)S(1)}, u32[]{:S(2)}) copy-start(f32[4,64,64]{2,1,0:T(8,128)S(1)} %reshape.14242) | copy-start | bytes 196612
  146.0 43.9 %copy-start.123 = (pred[64]{0:T(512)(128)(4,1)}, pred[64]{0:T(512)(128)(4,1)S(1)}, u32[]{:S(2)}) copy-start(pred[64]{0:T(512)(128)(4,1)S(1)} %iota_compare_fusion) | copy-start | bytes 196
  152.4 321.9 %copy-start.14 = (f32[5,64,64]{2,0,1:T(8,128)}, f32[5,64,64]{2,0,1:T(8,128)S(1)}, u32[]{:S(2)}) copy-start(f32[5,64,64]{2,0,1:T(8,128)S(1)} %copy.2823) | copy-start | bytes 245764
  162.5 8.5 %collective-permute-start = (f32[2,3,1,1,64,64]{5,3,4,2,1,0:T(1,128)S(1)}, f32[2,3,1,1,64,64]{5,3,4,2,1,0:T(1,128)S(1)}, u32[]{:S(2)}, u32[]{:S(2)}) collective-permute-start(f32[2,3,1,1,64,64]{5,3,4,2,1,0:T(1,128)S(1)} %get-tuple-element.141), channel_id=1, source_target_pairs={{0,1},{1,2},{2,3},{3,4},{4,5},{5,6},{6,7},{7,8},{8,9},{9,10},{10,1... | collective-permute-start | bytes 294920 | tf_op jit(solution)/shard_map/ppermute | solution.py:25
  166.5 22.2 %collective-permute-start.1 = (f32[2,3,1,1,64,64]{5,3,4,2,1,0:T(1,128)}, f32[2,3,1,1,64,64]{5,3,4,2,1,0:T(1,128)}, u32[]{:S(2)}, u32[]{:S(2)}) collective-permute-start(f32[2,3,1,1,64,64]{5,3,4,2,1,0:T(1,128)} %get-tuple-element.142), channel_id=1, source_target_pairs={{1,0},{2,1},{3,2},{4,3},{5,4},{6,5},{7,6},{8,7},{9,8},{10,9},{11,1... | collective-permute-start | bytes 294920 | tf_op jit(solution)/shard_map/ppermute | solution.py:26
  188.7 283.9 %copy-start.54 = (f32[1,3,1,1,64,64]{5,4,3,2,1,0:T(8,128)}, f32[1,3,1,1,64,64]{5,4,3,2,1,0:T(8,128)S(1)}, u32[]{:S(2)}) copy-start(f32[1,3,1,1,64,64]{5,4,3,2,1,0:T(8,128)S(1)} %mul.3410) | copy-start | bytes 147460
  398.3 41.0 %copy-start.43 = (f32[3,4,4096]{2,1,0:T(4,128)S(1)}, f32[3,4,4096]{2,1,0:T(4,128)}, u32[]{:S(2)}) copy-start(f32[3,4,4096]{2,1,0:T(4,128)} %reshape.14240) | copy-start | bytes 589828
  444.4 8.0 collective-permute-start.3
  444.4 28.2 %collective-permute-start.4 = (f32[2,3,1,1,64,64]{5,3,4,2,1,0:T(1,128)}, f32[2,3,1,1,64,64]{5,3,4,2,1,0:T(1,128)}, u32[]{:S(2)}, u32[]{:S(2)}) collective-permute-start(f32[2,3,1,1,64,64]{5,3,4,2,1,0:T(1,128)} %get-tuple-element.136), channel_id=1, source_target_pairs={{1,0},{2,1},{3,2},{4,3},{5,4},{6,5},{7,6},{8,7},{9,8},{10,9},{11,1... | collective-permute-start | bytes 294920 | tf_op jit(solution)/shard_map/ppermute | solution.py:26
  487.7 47.1 %copy-start.24 = (f32[1,3,1,4,4096]{4,3,1,2,0:T(4,128)S(1)}, f32[1,3,1,4,4096]{4,3,1,2,0:T(4,128)}, u32[]{:S(2)}) copy-start(f32[1,3,1,4,4096]{4,3,1,2,0:T(4,128)} %copy-done.23) | copy-start | bytes 589828
  487.7 47.1 %copy-start.27 = (f32[1,3,1,4,4096]{4,3,1,2,0:T(4,128)S(1)}, f32[1,3,1,4,4096]{4,3,1,2,0:T(4,128)}, u32[]{:S(2)}) copy-start(f32[1,3,1,4,4096]{4,3,1,2,0:T(4,128)} %copy-done.26) | copy-start | bytes 589828
  723.6 8.9 %collective-permute-start.5 = (f32[2,3,1,1,64,64]{5,3,4,2,1,0:T(1,128)S(1)}, f32[2,3,1,1,64,64]{5,3,4,2,1,0:T(1,128)S(1)}, u32[]{:S(2)}, u32[]{:S(2)}) collective-permute-start(f32[2,3,1,1,64,64]{5,3,4,2,1,0:T(1,128)S(1)} %copy.2808), channel_id=1, source_target_pairs={{0,1},{1,2},{2,3},{3,4},{4,5},{5,6},{6,7},{7,8},{8,9},{9,10},{10,1... | collective-permute-start | bytes 294920 | tf_op jit(solution)/shard_map/ppermute | solution.py:25
  727.9 22.4 %collective-permute-start.6 = (f32[2,3,1,1,64,64]{5,3,0,4,2,1:T(1,128)}, f32[2,3,1,1,64,64]{5,3,0,4,2,1:T(1,128)}, u32[]{:S(2)}, u32[]{:S(2)}) collective-permute-start(f32[2,3,1,1,64,64]{5,3,0,4,2,1:T(1,128)} %get-tuple-element.131), channel_id=1, source_target_pairs={{1,0},{2,1},{3,2},{4,3},{5,4},{6,5},{7,6},{8,7},{9,8},{10,9},{11,1... | collective-permute-start | bytes 294920 | tf_op jit(solution)/shard_map/ppermute | solution.py:26
  770.4 46.4 %copy-start.25 = (f32[1,3,1,4,4096]{4,3,1,2,0:T(4,128)S(1)}, f32[1,3,1,4,4096]{4,3,1,2,0:T(4,128)}, u32[]{:S(2)}) copy-start(f32[1,3,1,4,4096]{4,3,1,2,0:T(4,128)} %copy-done.23) | copy-start | bytes 589828
  770.4 46.4 %copy-start.28 = (f32[1,3,1,4,4096]{4,3,1,2,0:T(4,128)S(1)}, f32[1,3,1,4,4096]{4,3,1,2,0:T(4,128)}, u32[]{:S(2)}) copy-start(f32[1,3,1,4,4096]{4,3,1,2,0:T(4,128)} %copy-done.26) | copy-start | bytes 589828
  770.4 46.4 %copy-start.45 = (f32[1,3,1,4,4096]{4,3,1,2,0:T(4,128)S(1)}, f32[1,3,1,4,4096]{4,3,1,2,0:T(4,128)}, u32[]{:S(2)}) copy-start(f32[1,3,1,4,4096]{4,3,1,2,0:T(4,128)} %copy-done.44) | copy-start | bytes 589828
  770.4 46.4 %copy-start.47 = (f32[1,3,1,4,4096]{4,3,1,2,0:T(4,128)S(1)}, f32[1,3,1,4,4096]{4,3,1,2,0:T(4,128)}, u32[]{:S(2)}) copy-start(f32[1,3,1,4,4096]{4,3,1,2,0:T(4,128)} %copy-done.46) | copy-start | bytes 589828
  (115 other events, 287.4 us)
where the time goes:
time: 831 us; the launch traced here: 819 us
  local copies, waits for them, and re-layouts  320 us (39%)
  blocking collectives  225 us (27%)
  other arithmetic  140 us (17%)
  between operations  51.9 us (6%)
  matrix products  48.9 us (6%)
  starting transfers between devices  25.6 us (3%)
    unnamed x312, local copies, waits for them, and re-layouts  143 us
    psum x3, blocking collectives, on_device(): lax.psum((first_pair[0], first_pair[1], second_pair[0], second_pair[1]),...  97.3 us
    another operation x20, local copies, waits for them, and re-layouts, contract(): return jnp.stack([real_part, imag_part])  67.3 us
    psum x2, blocking collectives, on_device(): update_totals = lax.psum((update_pair[0], update_pair[1]), 'px')  66.5 us
    unnamed x5, other arithmetic  51.8 us
    all_to_all x4, local copies, waits for them, and re-layouts, precondition(): lax.all_to_all(flat_spectrum, 'px', split_axis=4, concat_axis=3, tiled=True)  46.9 us
    all_to_all x2, blocking collectives, precondition(): lax.all_to_all(worked, 'px', split_axis=3, concat_axis=4, tiled=True)  31 us
    all_to_all x2, blocking collectives, precondition(): lax.all_to_all(flat_spectrum, 'px', split_axis=4, concat_axis=3, tiled=True)  30.1 us
  transfers between devices with their start and end apart: 9, of which 2 were waited for; matrix products, arithmetic and copies ran while one was open for 23% of the time, Pallas kernels for 0%

commit v1 on v0

--- a/solution.py
+++ b/solution.py
@@ -257,7 +257,12 @@
         fields = contract(fields, forward_tables[2], "cvxyj,mj->cvxym")
         fields = contract(fields, forward_tables[1], "cvxjz,mj->cvxmz")
         flat_spectrum = fields.reshape(2, 3, vectors, planes, NG * NG)
-        gathered = lax.all_to_all(flat_spectrum, "px", split_axis=4, concat_axis=3, tiled=True)
+        gathered = jnp.concatenate(
+            lax.all_to_all(
+                jnp.stack(jnp.split(flat_spectrum, lax.axis_size("px"), axis=4)), "px", 0, 0
+            ),
+            axis=3,
+        )
         worked = column_work(gathered)
         returned = lax.all_to_all(worked, "px", split_axis=3, concat_axis=4, tiled=True)
         fields = returned.reshape(2, 3, vectors, planes, NG, NG)

time: 831 us -> 547 us (0.66)
  local copies, waits for them, and re-layouts: 320 us -> 96.1 us
  other arithmetic: 140 us -> 83.3 us
    unnamed x312 -> x370, local copies, waits for them, and re-layouts: 143 us -> 28.7 us
    another operation x20 -> x17, local copies, waits for them, and re-layouts: 67.3 us -> 5.87 us  [contract(): return jnp.stack([real_part, imag_part])]
    unnamed x5 -> x2, other arithmetic: 51.8 us -> 1.94 us
    all_to_all x4 -> x0, local copies, waits for them, and re-layouts: 46.9 us -> none  [precondition(): lax.all_to_all(flat_spectrum, 'px', split_axis=4, concat_axis=3, tiled=True)]
  transfers between devices with their start and end apart: 9 -> 9, of which waited for: 2 -> 2; matrix products, arithmetic and copies ran while one was open for 23% -> 19% of each run, Pallas kernels for 0% -> 0%
where the time goes in v1:
time: 547 us; the launch traced here: 537 us
  blocking collectives  224 us (41%)
  local copies, waits for them, and re-layouts  96.1 us (18%)
  other arithmetic  83.3 us (15%)
  between operations  53.2 us (10%)
  matrix products  47.1 us (9%)
  starting transfers between devices  25.9 us (5%)
  waiting for transfers between devices  7.59 us (1%)
    psum x3, blocking collectives, on_device(): lax.psum((first_pair[0], first_pair[1], second_pair[0], second_pair[1]),...  96.7 us
    psum x2, blocking collectives, on_device(): update_totals = lax.psum((update_pair[0], update_pair[1]), 'px')  66.4 us
    all_to_all x2, blocking collectives, precondition(): lax.all_to_all(worked, 'px', split_axis=3, concat_axis=4, tiled=True)  31.1 us
    another operation x46, other arithmetic, rotate(): jnp.stack([cosine * fields[0] - sine_part * fields[1], sine_part * fields...  29.8 us
    all_to_all x2, blocking collectives, precondition(): lax.all_to_all(jnp.stack(jnp.split(flat_spectrum, lax.axis_size('px'), ax...  29.6 us
    unnamed x370, local copies, waits for them, and re-layouts  28.7 us
    ppermute x3, starting transfers between devices, padded(): after = lax.ppermute(first, axis, down)  14.2 us
    concatenate x19, local copies, waits for them, and re-layouts, forward_step(): rolled = jnp.roll(fields, -1, along)  12.3 us
  transfers between devices with their start and end apart: 9, of which 2 were waited for; matrix products, arithmetic and copies ran while one was open for 19% of the time, Pallas kernels for 0%

profile of v1, /device:TPU:0, one launch (start us, length us, event | category | flops | bytes accessed | tf_op | source)
XLA Modules:
  0.0 536.8 jit_solution(8331032072989929378)
XLA Ops:
  2.0 1.4 fusion.759
  27.2 7.2 %all-to-all-start = ((f32[16,2,3,1,4,256]{5,4,2,1,3,0:T(4,128)}), f32[16,2,3,1,4,256]{5,4,2,1,3,0:T(4,128)S(1)}, u32[]{:S(2)}, u32[]{:S(2)}) async-start(f32[16,2,3,1,4,256]{5,4,2,1,3,0:T(4,128)} %constant_dynamic-update-slice_fusion.2), calls=%async_computation | async-start | bytes 786432 | tf_op jit(solution)/shard_map/all_to_all | solution.py:261
  41.8 4.8 all-to-all-done
  52.3 3.8 all-to-all-start.1
  56.1 1.9 select_add_fusion
  63.2 2.0 fusion.340
  65.4 2.8 all-to-all-done.1
  75.4 2.2 subtract_bitcast_fusion
  78.7 4.7 collective-permute-start.1
  98.6 1.4 subtract_bitcast_fusion.5
  101.2 1.9 fusion.47
  113.7 1.6 maximum_select_fusion.12
  123.7 32.4 %all-reduce.4 = (f32[1,1]{1,0:T(1,128)}, f32[1,1]{1,0:T(1,128)}, f32[1,1]{1,0:T(1,128)}, f32[1,1]{1,0:T(1,128)}) all-reduce(f32[1,1]{1,0:T(1,128)} %bitcast.289, f32[1,1]{1,0:T(1,128)} %bitcast.286, f32[1,1]{1,0:T(1,128)} %bitcast.290, f32[1,1]{1,0:T(1,128)} %bitcast.184), channel_id=1, replica_groups=mesh['kpt'=2,'px'=16] {'px'}, use_global_device_ids=true, to_apply=%region_3.4 | all-reduce | flops 4 | bytes 32 | tf_op jit(solution)/shard_map/psum | solution.py:290
  158.7 1.4 maximum_subtract_fusion.9
  170.4 14.8 %all_to_all.60 = f32[16,2,3,1,4,256]{5,4,2,1,3,0:T(4,128)S(1)} all-to-all(f32[16,2,3,1,4,256]{5,4,2,1,3,0:T(4,128)S(1)} %constant_dynamic-update-slice_fusion.20), channel_id=1, replica_groups=mesh['kpt'=2,'px'=16] {'px'}, dimensions={0} | all-to-all | bytes 786432 | tf_op jit(solution)/shard_map/all_to_all | solution.py:261
  190.2 15.5 %all_to_all.61 = f32[2,3,1,64,256]{4,0,2,1,3:T(2,128)S(1)} all-to-all(f32[2,3,1,64,256]{4,0,2,1,3:T(2,128)S(1)} %copy.2311), channel_id=1, replica_groups=mesh['kpt'=2,'px'=16] {'px'}, dimensions={3} | all-to-all | bytes 786432 | tf_op jit(solution)/shard_map/all_to_all | solution.py:267
  216.0 33.2 %all-reduce.3 = (f32[1,1]{1,0:T(1,128)}, f32[1,1]{1,0:T(1,128)}) all-reduce(f32[1,1]{1,0:T(1,128)} %bitcast.395, f32[1,1]{1,0:T(1,128)} %bitcast.394), channel_id=1, replica_groups=mesh['kpt'=2,'px'=16] {'px'}, use_global_device_ids=true, to_apply=%region_6.7 | all-reduce | flops 2 | bytes 16 | tf_op jit(solution)/shard_map/psum | solution.py:297
  256.9 4.8 collective-permute-start.4
  277.0 1.7 copy.2351
  278.7 1.7 copy.2342
  280.5 1.4 subtract_bitcast_fusion.4
  308.5 32.2 %all-reduce.2 = (f32[1,1]{1,0:T(1,128)}, f32[1,1]{1,0:T(1,128)}, f32[1,1]{1,0:T(1,128)}, f32[1,1]{1,0:T(1,128)}) all-reduce(f32[1,1]{1,0:T(1,128)} %bitcast.496, f32[1,1]{1,0:T(1,128)} %bitcast.491, f32[1,1]{1,0:T(1,128)} %bitcast.499, f32[1,1]{1,0:T(1,128)} %bitcast.408), channel_id=1, replica_groups=mesh['kpt'=2,'px'=16] {'px'}, use_global_device_ids=true, to_apply=%region_9.10 | all-reduce | flops 4 | bytes 32 | tf_op jit(solution)/shard_map/psum | solution.py:290
  343.3 1.4 maximum_subtract_fusion.10
  355.3 14.8 %all_to_all.62 = f32[16,2,3,1,4,256]{5,4,2,1,3,0:T(4,128)S(1)} all-to-all(f32[16,2,3,1,4,256]{5,4,2,1,3,0:T(4,128)S(1)} %constant_dynamic-update-slice_fusion.38), channel_id=1, replica_groups=mesh['kpt'=2,'px'=16] {'px'}, dimensions={0} | all-to-all | bytes 786432 | tf_op jit(solution)/shard_map/all_to_all | solution.py:261
  375.1 15.5 %all_to_all.63 = f32[2,3,1,64,256]{4,0,2,1,3:T(2,128)S(1)} all-to-all(f32[2,3,1,64,256]{4,0,2,1,3:T(2,128)S(1)} %copy.2428), channel_id=1, replica_groups=mesh['kpt'=2,'px'=16] {'px'}, dimensions={3} | all-to-all | bytes 786432 | tf_op jit(solution)/shard_map/all_to_all | solution.py:267
  397.6 1.8 multiply_reduce_fusion.2
  402.0 33.2 %all-reduce.1 = (f32[1,1]{1,0:T(1,128)}, f32[1,1]{1,0:T(1,128)}) all-reduce(f32[1,1]{1,0:T(1,128)} %bitcast.591, f32[1,1]{1,0:T(1,128)} %bitcast.590), channel_id=1, replica_groups=mesh['kpt'=2,'px'=16] {'px'}, use_global_device_ids=true, to_apply=%region_12.13 | all-reduce | flops 2 | bytes 16 | tf_op jit(solution)/shard_map/psum | solution.py:297
  447.4 4.6 collective-permute-start.6
  463.9 1.6 maximum_select_fusion.8
  467.3 1.9 copy.2970
  471.5 2.3 fusion.56
  494.8 32.2 %all-reduce = (f32[1,1]{1,0:T(1,128)}, f32[1,1]{1,0:T(1,128)}, f32[1,1]{1,0:T(1,128)}, f32[1,1]{1,0:T(1,128)}) all-reduce(f32[1,1]{1,0:T(1,128)} %bitcast.679, f32[1,1]{1,0:T(1,128)} %bitcast.674, f32[1,1]{1,0:T(1,128)} %bitcast.682, f32[1,1]{1,0:T(1,128)} %bitcast.604), channel_id=1, replica_groups=mesh['kpt'=2,'px'=16] {'px'}, use_global_device_ids=true, to_apply=%region_15.16 | all-reduce | flops 4 | bytes 32 | tf_op jit(solution)/shard_map/psum | solution.py:290
  (787 shorter events, 199.8 us)
Async XLA Ops:
  1.5 61.7 %collective-permute-start.2 = (s32[1,4096]{1,0:T(1,128)S(1)}, s32[1,4096]{1,0:T(1,128)S(1)}, u32[]{:S(2)}, u32[]{:S(2)}) collective-permute-start(s32[1,4096]{1,0:T(1,128)S(1)} %slice.1041), channel_id=1, source_target_pairs={{0,1},{1,2},{2,3},{3,4},{4,5},{5,6},{6,7},{7,8},{8,9},{9,10},{10,1... | collective-permute-start | bytes 49160 | tf_op jit(solution)/shard_map/ppermute | solution.py:15
  4.1 207.8 %copy-start.95 = (f32[64]{0:T(128)}, f32[64]{0:T(128)S(1)}, u32[]{:S(2)}) copy-start(f32[64]{0:T(128)S(1)} %multiply_multiply_fusion) | copy-start | bytes 772
  8.7 200.6 %copy-start.97 = (f32[64]{0:T(128)}, f32[64]{0:T(128)S(1)}, u32[]{:S(2)}) copy-start(f32[64]{0:T(128)S(1)} %multiply_multiply_fusion.2) | copy-start | bytes 772
  17.1 17.3 %copy-start.144 = (f32[3]{0:T(128)S(1)}, f32[3]{0:T(128)}, u32[]{:S(2)}) copy-start(f32[3]{0:T(128)} %param.7) | copy-start | bytes 40
  17.1 18.5 %copy-start.145 = (f32[2]{0:T(128)S(1)}, f32[2]{0:T(128)}, u32[]{:S(2)}) copy-start(f32[2]{0:T(128)} %param.9) | copy-start | bytes 28
  27.2 19.4 %all-to-all-start = ((f32[16,2,3,1,4,256]{5,4,2,1,3,0:T(4,128)}), f32[16,2,3,1,4,256]{5,4,2,1,3,0:T(4,128)S(1)}, u32[]{:S(2)}, u32[]{:S(2)}) async-start(f32[16,2,3,1,4,256]{5,4,2,1,3,0:T(4,128)} %constant_dynamic-update-slice_fusion.2), calls=%async_computation | async-start | bytes 786432 | tf_op jit(solution)/shard_map/all_to_all | solution.py:261
  37.6 11.3 %copy-start.134 = (f32[64]{0:T(128)}, f32[64]{0:T(128)S(1)}, u32[]{:S(2)}) copy-start(f32[64]{0:T(128)S(1)} %get-tuple-element.316) | copy-start | bytes 772
  37.6 11.3 %copy-start.137 = (f32[64]{0:T(128)}, f32[64]{0:T(128)S(1)}, u32[]{:S(2)}) copy-start(f32[64]{0:T(128)S(1)} %get-tuple-element.317) | copy-start | bytes 772
  38.3 10.6 %copy-start.140 = (f32[64]{0:T(128)}, f32[64]{0:T(128)S(1)}, u32[]{:S(2)}) copy-start(f32[64]{0:T(128)S(1)} %get-tuple-element.319) | copy-start | bytes 772
  38.3 151.0 %copy-start.99 = (f32[64]{0:T(128)}, f32[64]{0:T(128)S(1)}, u32[]{:S(2)}) copy-start(f32[64]{0:T(128)S(1)} %get-tuple-element.318) | copy-start | bytes 772
  39.7 9.3 %copy-start.112 = (f32[256]{0:T(256)}, f32[256]{0:T(256)S(1)}, u32[]{:S(2)}) copy-start(f32[256]{0:T(256)S(1)} %get-tuple-element.320) | copy-start | bytes 3076
  39.7 147.9 %copy-start.110 = (f32[256]{0:T(256)}, f32[256]{0:T(256)S(1)}, u32[]{:S(2)}) copy-start(f32[256]{0:T(256)S(1)} %get-tuple-element.321) | copy-start | bytes 3076
  40.4 8.6 %copy-start.115 = (f32[256]{0:T(256)}, f32[256]{0:T(256)S(1)}, u32[]{:S(2)}) copy-start(f32[256]{0:T(256)S(1)} %get-tuple-element.312) | copy-start | bytes 3076
  40.4 8.6 %copy-start.118 = (f32[256]{0:T(256)}, f32[256]{0:T(256)S(1)}, u32[]{:S(2)}) copy-start(f32[256]{0:T(256)S(1)} %get-tuple-element.313) | copy-start | bytes 3076
  41.1 7.9 %copy-start.124 = (f32[256]{0:T(256)}, f32[256]{0:T(256)S(1)}, u32[]{:S(2)}) copy-start(f32[256]{0:T(256)S(1)} %get-tuple-element.315) | copy-start | bytes 3076
  52.3 15.9 %all-to-all-start.1 = ((f32[2,3,1,64,256]{4,0,2,1,3:T(2,128)}), f32[2,3,1,64,256]{4,0,2,1,3:T(2,128)S(1)}, u32[]{:S(2)}, u32[]{:S(2)}) async-start(f32[2,3,1,64,256]{4,0,2,1,3:T(2,128)} %copy.2190), calls=%async_computation.1 | async-start | bytes 786432 | tf_op jit(solution)/shard_map/all_to_all | solution.py:267
  58.2 57.5 %copy-start.20 = (f32[4,64,64]{2,1,0:T(8,128)}, f32[4,64,64]{2,1,0:T(8,128)S(1)}, u32[]{:S(2)}) copy-start(f32[4,64,64]{2,1,0:T(8,128)S(1)} %reshape.14255) | copy-start | bytes 196612
  58.9 42.3 %copy-start.131 = (pred[64]{0:T(512)(128)(4,1)}, pred[64]{0:T(512)(128)(4,1)S(1)}, u32[]{:S(2)}) copy-start(pred[64]{0:T(512)(128)(4,1)S(1)} %iota_compare_fusion) | copy-start | bytes 196
  65.4 220.5 %copy-start.14 = (f32[5,64,64]{2,0,1:T(8,128)}, f32[5,64,64]{2,0,1:T(8,128)S(1)}, u32[]{:S(2)}) copy-start(f32[5,64,64]{2,0,1:T(8,128)S(1)} %copy.2809) | copy-start | bytes 245764
  75.3 8.1 %collective-permute-start = (f32[2,3,1,1,64,64]{5,3,4,2,1,0:T(1,128)S(1)}, f32[2,3,1,1,64,64]{5,3,4,2,1,0:T(1,128)S(1)}, u32[]{:S(2)}, u32[]{:S(2)}) collective-permute-start(f32[2,3,1,1,64,64]{5,3,4,2,1,0:T(1,128)S(1)} %get-tuple-element.139), channel_id=1, source_target_pairs={{0,1},{1,2},{2,3},{3,4},{4,5},{5,6},{6,7},{7,8},{8,9},{9,10},{10,1... | collective-permute-start | bytes 294920 | tf_op jit(solution)/shard_map/ppermute | solution.py:25
  78.7 21.3 %collective-permute-start.1 = (f32[2,3,1,1,64,64]{5,3,4,2,1,0:T(1,128)}, f32[2,3,1,1,64,64]{5,3,4,2,1,0:T(1,128)}, u32[]{:S(2)}, u32[]{:S(2)}) collective-permute-start(f32[2,3,1,1,64,64]{5,3,4,2,1,0:T(1,128)} %get-tuple-element.140), channel_id=1, source_target_pairs={{1,0},{2,1},{3,2},{4,3},{5,4},{6,5},{7,6},{8,7},{9,8},{10,9},{11,1... | collective-permute-start | bytes 294920 | tf_op jit(solution)/shard_map/ppermute | solution.py:26
  256.9 8.3 %collective-permute-start.3 = (f32[2,3,1,1,64,64]{5,3,4,2,1,0:T(1,128)S(1)}, f32[2,3,1,1,64,64]{5,3,4,2,1,0:T(1,128)S(1)}, u32[]{:S(2)}, u32[]{:S(2)}) collective-permute-start(f32[2,3,1,1,64,64]{5,3,4,2,1,0:T(1,128)S(1)} %get-tuple-element.133), channel_id=1, source_target_pairs={{0,1},{1,2},{2,3},{3,4},{4,5},{5,6},{6,7},{7,8},{8,9},{9,10},{10,1... | collective-permute-start | bytes 294920 | tf_op jit(solution)/shard_map/ppermute | solution.py:25
  256.9 26.9 %collective-permute-start.4 = (f32[2,3,1,1,64,64]{5,3,4,2,1,0:T(1,128)}, f32[2,3,1,1,64,64]{5,3,4,2,1,0:T(1,128)}, u32[]{:S(2)}, u32[]{:S(2)}) collective-permute-start(f32[2,3,1,1,64,64]{5,3,4,2,1,0:T(1,128)} %get-tuple-element.134), channel_id=1, source_target_pairs={{1,0},{2,1},{3,2},{4,3},{5,4},{6,5},{7,6},{8,7},{9,8},{10,9},{11,1... | collective-permute-start | bytes 294920 | tf_op jit(solution)/shard_map/ppermute | solution.py:26
  301.2 46.8 %copy-start.23 = (f32[1,3,1,4,4096]{4,3,1,2,0:T(4,128)S(1)}, f32[1,3,1,4,4096]{4,3,1,2,0:T(4,128)}, u32[]{:S(2)}) copy-start(f32[1,3,1,4,4096]{4,3,1,2,0:T(4,128)} %copy-done.22) | copy-start | bytes 589828
  301.3 46.8 %copy-start.26 = (f32[1,3,1,4,4096]{4,3,1,2,0:T(4,128)S(1)}, f32[1,3,1,4,4096]{4,3,1,2,0:T(4,128)}, u32[]{:S(2)}) copy-start(f32[1,3,1,4,4096]{4,3,1,2,0:T(4,128)} %copy-done.25) | copy-start | bytes 589828
  355.0 15.3 %copy-start.100 = (f32[64]{0:T(128)S(1)}, f32[64]{0:T(128)}, u32[]{:S(2)}) copy-start(f32[64]{0:T(128)} %copy-done.99) | copy-start | bytes 772
  443.0 9.0 %collective-permute-start.5 = (f32[2,3,1,1,64,64]{5,3,4,2,1,0:T(1,128)S(1)}, f32[2,3,1,1,64,64]{5,3,4,2,1,0:T(1,128)S(1)}, u32[]{:S(2)}, u32[]{:S(2)}) collective-permute-start(f32[2,3,1,1,64,64]{5,3,4,2,1,0:T(1,128)S(1)} %copy.2794), channel_id=1, source_target_pairs={{0,1},{1,2},{2,3},{3,4},{4,5},{5,6},{6,7},{7,8},{8,9},{9,10},{10,1... | collective-permute-start | bytes 294920 | tf_op jit(solution)/shard_map/ppermute | solution.py:25
  447.4 23.0 %collective-permute-start.6 = (f32[2,3,1,1,64,64]{5,3,0,4,2,1:T(1,128)}, f32[2,3,1,1,64,64]{5,3,0,4,2,1:T(1,128)}, u32[]{:S(2)}, u32[]{:S(2)}) collective-permute-start(f32[2,3,1,1,64,64]{5,3,0,4,2,1:T(1,128)} %get-tuple-element.129), channel_id=1, source_target_pairs={{1,0},{2,1},{3,2},{4,3},{5,4},{6,5},{7,6},{8,7},{9,8},{10,9},{11,1... | collective-permute-start | bytes 294920 | tf_op jit(solution)/shard_map/ppermute | solution.py:26
  487.8 46.6 %copy-start.24 = (f32[1,3,1,4,4096]{4,3,1,2,0:T(4,128)S(1)}, f32[1,3,1,4,4096]{4,3,1,2,0:T(4,128)}, u32[]{:S(2)}) copy-start(f32[1,3,1,4,4096]{4,3,1,2,0:T(4,128)} %copy-done.22) | copy-start | bytes 589828
  487.8 46.6 %copy-start.27 = (f32[1,3,1,4,4096]{4,3,1,2,0:T(4,128)S(1)}, f32[1,3,1,4,4096]{4,3,1,2,0:T(4,128)}, u32[]{:S(2)}) copy-start(f32[1,3,1,4,4096]{4,3,1,2,0:T(4,128)} %copy-done.25) | copy-start | bytes 589828
  487.8 46.6 %copy-start.42 = (f32[1,3,1,4,4096]{4,3,1,2,0:T(4,128)S(1)}, f32[1,3,1,4,4096]{4,3,1,2,0:T(4,128)}, u32[]{:S(2)}) copy-start(f32[1,3,1,4,4096]{4,3,1,2,0:T(4,128)} %copy-done.41) | copy-start | bytes 589828
  487.8 46.6 %copy-start.44 = (f32[1,3,1,4,4096]{4,3,1,2,0:T(4,128)S(1)}, f32[1,3,1,4,4096]{4,3,1,2,0:T(4,128)}, u32[]{:S(2)}) copy-start(f32[1,3,1,4,4096]{4,3,1,2,0:T(4,128)} %copy-done.43) | copy-start | bytes 589828
  (123 other events, 230.3 us)
